TPU v7x, 32 devices: a whole 2x2x4 slice. The times are simulated.
32 devices in a mesh: px: 8 (over z, y), py: 4 (over x, core).
Axes of the slice: x: 2, y: 2, z: 4, core: 2. Of those that a mesh axis runs over, the one named last changes fastest.
Arguments:
- field: bfloat16 [1, 32, 128, 128, 256], P(None, None, 'px', 'py'), may hold values from -6 to 6
- spectral_weight: bfloat16 [2, 32, 32, 32, 64, 64], P(None, None, 'px', 'py'), may hold values from -72 to 72
- point_weight: bfloat16 [32, 32], replicated, may hold values from -1 to 1
- point_bias: float32 [32], replicated, may hold values from -3 to 3
Outputs:
- layer_out: bfloat16 [1, 32, 128, 128, 256], P(None, None, 'px', 'py')
All inputs are finite; a program needn't handle non-finite values.
Results may differ from a plain program's by a relative error of at most 0.0085.
Values may be sent and summed in bfloat16 or wider, within the bound.
A program may use at most 192 MiB of HBM per device.

v0:
```python
from functools import partial
import math
import jax
import jax.numpy as jnp
from jax import lax
from jax.sharding import PartitionSpec as P

MX = 64
MY = 64
MZ = 32


def contract(form, left, right):
    return jnp.einsum(
        form, left, right, precision=lax.Precision.HIGHEST, preferred_element_type=jnp.float32
    )


def angle_table(length, count, signed):
    position = jnp.arange(length, dtype=jnp.int32)
    number = jnp.arange(count, dtype=jnp.int32)
    if signed:
        number = jnp.where(number < count // 2, number, number - count)
    product = position[:, None] * number[None, :] % length
    return 2.0 * math.pi / length * product.astype(jnp.float32)


def forward_x(piece, keep_count, cos_x, sin_x):
    real_part = piece[0]
    imag_part = piece[1]
    out_real = contract("ix,bcxm->bcim", cos_x, real_part) + contract(
        "ix,bcxm->bcim", sin_x, imag_part
    )
    out_imag = contract("ix,bcxm->bcim", cos_x, imag_part) - contract(
        "ix,bcxm->bcim", sin_x, real_part
    )
    return jnp.stack([out_real, out_imag], axis=0)


def inverse_z(piece, table):
    return contract("pbcxky,pkz->bcxyz", piece, table)


def body(field, spectral_weight, point_weight, point_bias):
    batch, channels, rows_x, rows_y, depth = field.shape
    grid_x = rows_x * lax.axis_size("px")
    grid_y = rows_y * lax.axis_size("py")
    theta_x = angle_table(grid_x, MX, True)
    theta_y = angle_table(grid_y, MY, True)
    wide = field.astype(jnp.float32)
    count = MZ
    theta_z = angle_table(depth, count, False)
    z_real = contract("bcxyz,zk->bcxky", wide, jnp.cos(theta_z))
    z_imag = contract("bcxyz,zk->bcxky", wide, -jnp.sin(theta_z))
    along_z = jnp.stack([z_real, z_imag], axis=0).reshape(
        2, batch, channels, rows_x, count * rows_y
    )
    step_x = partial(
        forward_x, keep_count=MZ * rows_y, cos_x=jnp.cos(theta_x).T, sin_x=jnp.sin(theta_x).T
    )
    along_x = step_x(lax.all_to_all(along_z, "px", split_axis=2, concat_axis=3, tiled=True))
    shape = along_x.shape
    along_x = along_x.reshape(shape[0], shape[1], shape[2], shape[3], MZ, rows_y)
    moved = lax.all_to_all(along_x, "py", split_axis=4, concat_axis=5, tiled=True)
    cos_y = jnp.cos(theta_y)
    sin_y = jnp.sin(theta_y)
    spec_real = contract("bciky,yj->bcikj", moved[0], cos_y) + contract(
        "bciky,yj->bcikj", moved[1], sin_y
    )
    spec_imag = contract("bciky,yj->bcikj", moved[1], cos_y) - contract(
        "bciky,yj->bcikj", moved[0], sin_y
    )
    spectrum = jnp.stack([spec_real, spec_imag], axis=0).astype(jnp.bfloat16)
    gathered = lax.all_gather(spectrum, "px", axis=2, tiled=True)
    in_real = gathered[0].astype(jnp.float32)
    in_imag = gathered[1].astype(jnp.float32)
    weight_real = spectral_weight[0].astype(jnp.float32)
    weight_imag = spectral_weight[1].astype(jnp.float32)
    mixed_real = contract("bcikj,cokij->boikj", in_real, weight_real) - contract(
        "bcikj,cokij->boikj", in_imag, weight_imag
    )
    mixed_imag = contract("bcikj,cokij->boikj", in_real, weight_imag) + contract(
        "bcikj,cokij->boikj", in_imag, weight_real
    )
    cos_yt = jnp.cos(theta_y).T
    sin_yt = jnp.sin(theta_y).T
    back_real = contract("boikj,jy->boiky", mixed_real, cos_yt) - contract(
        "boikj,jy->boiky", mixed_imag, sin_yt
    )
    back_imag = contract("boikj,jy->boiky", mixed_real, sin_yt) + contract(
        "boikj,jy->boiky", mixed_imag, cos_yt
    )
    returned = lax.all_to_all(
        jnp.stack([back_real, back_imag], axis=0), "py", split_axis=5, concat_axis=4, tiled=True
    )
    cos_xt = jnp.cos(theta_x)
    sin_xt = jnp.sin(theta_x)
    out_real = contract("xi,boiky->boxky", cos_xt, returned[0]) - contract(
        "xi,boiky->boxky", sin_xt, returned[1]
    )
    out_imag = contract("xi,boiky->boxky", sin_xt, returned[0]) + contract(
        "xi,boiky->boxky", cos_xt, returned[1]
    )
    planes = jnp.stack([out_real, out_imag], axis=0)
    theta_back = angle_table(depth, MZ, False).T
    factor = jnp.where(jnp.arange(MZ) == 0, 1.0, 2.0).astype(jnp.float32) / float(
        grid_x * grid_y * depth
    )
    table_back = jnp.stack(
        [factor[:, None] * jnp.cos(theta_back), -factor[:, None] * jnp.sin(theta_back)], axis=0
    )
    spectral = inverse_z(
        lax.all_to_all(planes, "px", split_axis=3, concat_axis=2, tiled=True), table=table_back
    )
    pointwise = jnp.einsum(
        "oc,bcxyz->boxyz", point_weight, field, preferred_element_type=jnp.float32
    )
    pointwise = pointwise + point_bias[None, :, None, None, None]
    return jax.nn.gelu(spectral + pointwise, approximate=False).astype(jnp.bfloat16)


def solution(mesh):
    placed = (P(None, None, "px", "py", None), P(None, None, "px", "py", None, None), P(), P())
    return jax.shard_map(
        body, mesh=mesh, in_specs=placed, out_specs=P(None, None, "px", "py", None), check_vma=False
    )
```

profile of v0, /device:TPU:0, one launch (start us, length us, event | category | flops | bytes accessed | tf_op | source)
XLA Modules:
  0.0 746.2 jit_solution(797422356262062606)
XLA Ops:
  6.5 24.2 %convolution_bitcast_fusion.1 = f32[1,32,16,32,32]{4,3,2,1,0:T(8,128)} fusion(bf16[1,32,16,32,256]{4,3,2,1,0:T(8,128)(2,1)} %param.4), kind=kOutput, calls=%fused_computation.41 | convolution fusion | flops 1610727424 | bytes 10485760 | tf_op jit(solution)/shard_map/bcxyz,zk->bcxky/dot_general | solution.py:14
  30.8 21.1 %convolution_bitcast_fusion = f32[1,32,16,32,32]{4,3,2,1,0:T(8,128)} fusion(bf16[1,32,16,32,256]{4,3,2,1,0:T(8,128)(2,1)S(1)} %copy-done.2), kind=kOutput, calls=%fused_computation.40 | convolution fusion | flops 1610735616 | bytes 10485760 | tf_op jit(solution)/shard_map/bcxyz,zk->bcxky/dot_general | solution.py:14
  51.9 6.6 stack.50
  58.6 7.9 %stack.51 = f32[1,1,32,16,1024]{4,3,2,1,0:T(8,128)} reshape(f32[1,32,16,32,32]{4,3,2,1,0:T(8,128)} %convolution_bitcast_fusion) | data formatting | bytes 4194304 | tf_op jit(solution)/shard_map/stack | solution.py:55
  66.5 4.4 pad_maximum_fusion
  70.8 7.3 all-to-all-start
  78.2 93.2 %all-to-all-done = f32[2,1,32,16,1024]{4,3,1,0,2:T(8,128)} async-done(((f32[2,1,32,16,1024]{4,3,1,0,2:T(8,128)}), f32[2,1,32,16,1024]{4,3,1,0,2:T(8,128)}, u32[]{:S(2)}, u32[]{:S(2)}) %all-to-all-start) | async-done | bytes 4194336 | tf_op jit(solution)/shard_map/all_to_all | solution.py:61
  185.5 4.4 copy_bitcast_fusion.2
  189.9 4.5 reshape.325
  194.4 28.9 %all_to_all.60 = f32[4,1,131072]{2,1,0:T(1,128)} all-to-all(f32[4,1,131072]{2,1,0:T(1,128)S(1)} %reshape.325), channel_id=1, replica_groups=mesh['px'=8,'py'=4] {'py'}, dimensions={0} | all-to-all | bytes 4194304 | tf_op jit(solution)/shard_map/all_to_all | solution.py:64
  223.9 7.7 %reduce.8 = f32[4,131072]{1,0:T(4,128)S(1)} reduce(f32[4,1,131072]{2,1,0:T(1,128)} %all_to_all.60, f32[]{:T(128)} %broadcast.331), dimensions={1}, to_apply=%all_to_all.47.reduce_sub_computation | reduce | bytes 4194308 | tf_op jit(solution)/shard_map/all_to_all | solution.py:64
  231.6 4.0 reshape.326
  249.4 122.7 %all-gather.2.cloned.1.call-done = bf16[2,1,32,64,8,64]{5,4,3,2,1,0:T(8,128)(2,1)} async-done(((bf16[2,1,4,64,8,64]{5,4,3,2,1,0:T(8,128)(2,1)}), bf16[2,1,32,64,8,64]{5,4,3,2,1,0:T(8,128)(2,1)}) %all-gather.2.cloned.1.call-update) | async-done | bytes 4194320 | tf_op jit(solution)/shard_map/all_gather | solution.py:74
  372.1 11.7 %fusion.16 = (f32[64,8,64,32]{2,1,0,3:T(8,128)}, f32[64,8,64,32]{2,1,0,3:T(8,128)}) fusion(bf16[2,1,32,64,8,64]{5,4,3,2,1,0:T(8,128)(2,1)} %all-gather.2.cloned.1.call-done), kind=kLoop, calls=%fused_computation.32 | loop fusion | flops 2097152 | bytes 12582912
  383.8 8.4 %copy.107 = f32[64,8,64,32]{2,0,1,3:T(8,128)} copy(f32[64,8,64,32]{2,1,0,3:T(8,128)} %get-tuple-element.11) | data formatting | bytes 8388608
  392.2 5.0 copy.106
  397.2 23.1 %fusion.3 = (f32[64,8,64,4]{2,0,1,3:T(8,128)S(1)}, f32[64,8,64,4]{2,0,1,3:T(8,128)S(1)}, f32[64,8,64,4]{2,0,1,3:T(8,128)}, f32[64,8,64,4]{2,0,1,3:T(8,128)S(1)}) fusion(f32[64,8,64,32]{2,0,1,3:T(8,128)} %copy.106, bf16[2,32,4,8,64,64]{5,4,3,2,1,0:T(8,128)(2,1)} %param.5, f32[64,8,64,32]{2,0,1,3:T(8,128)} %copy.107), kind=kLoop, calls=%fused_computation.7 | loop fusion | flops 41418752 | bytes 27262976
  432.8 4.7 copy.58
  437.5 4.5 reshape.327
  442.0 28.9 %all_to_all.61 = f32[4,1,131072]{2,1,0:T(1,128)} all-to-all(f32[4,1,131072]{2,1,0:T(1,128)S(1)} %reshape.327), channel_id=1, replica_groups=mesh['px'=8,'py'=4] {'py'}, dimensions={0} | all-to-all | bytes 4194304 | tf_op jit(solution)/shard_map/all_to_all | solution.py:93
  470.9 7.7 %reduce.9 = f32[4,131072]{1,0:T(4,128)S(1)} reduce(f32[4,1,131072]{2,1,0:T(1,128)} %all_to_all.61, f32[]{:T(128)} %broadcast.331), dimensions={1}, to_apply=%all_to_all.50.reduce_sub_computation | reduce | bytes 4194308 | tf_op jit(solution)/shard_map/all_to_all | solution.py:93
  482.6 4.6 copy.59
  499.7 14.4 %copy.62 = f32[2,1,4,128,32,32]{5,4,2,1,0,3:T(8,128)} copy(f32[2,1,4,128,32,32]{3,5,4,2,1,0:T(8,128)} %pad_maximum_fusion.2) | data formatting | bytes 8388608 | tf_op jit(solution)/shard_map/stack | solution.py:104
  514.0 12.8 %reshape.329 = f32[8,1,131072]{2,1,0:T(1,128)} reshape(f32[128,2,1,4,32,32]{5,4,3,2,1,0:T(8,128)} %bitcast.215) | data formatting | bytes 8388608
  526.9 4.8 all-to-all-start.3
  531.8 14.2 %fusion.14 = f32[16,32,256,32]{2,3,1,0:T(8,128)} fusion(bf16[32,16,32,256]{3,2,1,0:T(8,128)(2,1)} %bitcast.214, bf16[32,32]{1,0:T(8,128)(2,1)S(1)} %copy-done), kind=kOutput, calls=%fused_computation.29 | convolution fusion | flops 268435456 | bytes 25167872 | tf_op jit(solution)/shard_map/oc,bcxyz->boxyz/dot_general | solution.py:115
  546.0 78.7 %all-to-all-done.3 = f32[8,1,131072]{2,1,0:T(1,128)} async-done(((f32[8,1,131072]{2,1,0:T(1,128)}), f32[8,1,131072]{2,1,0:T(1,128)}, u32[]{:S(2)}, u32[]{:S(2)}) %all-to-all-start.3) | async-done | bytes 4194336 | tf_op jit(solution)/shard_map/all_to_all | solution.py:113
  624.7 14.9 %reduce.10 = f32[8,131072]{1,0:T(8,128)} reduce(f32[8,1,131072]{2,1,0:T(1,128)} %all-to-all-done.3, f32[]{:T(128)} %broadcast.331), dimensions={1}, to_apply=%all_to_all.53.reduce_sub_computation | reduce | bytes 8388612 | tf_op jit(solution)/shard_map/all_to_all | solution.py:113
  639.6 13.3 %reshape.330 = f32[128,2,1,4,32,32]{5,4,3,2,1,0:T(8,128)} reshape(f32[8,131072]{1,0:T(8,128)} %reduce.10) | data formatting | bytes 8388608
  653.0 11.8 %copy.63 = f32[2,1,4,128,32,32]{5,4,3,2,0,1:T(8,128)} copy(f32[2,1,4,128,32,32]{5,4,2,1,0,3:T(8,128)} %bitcast.216) | data formatting | bytes 8388608 | tf_op jit(solution)/shard_map/all_to_all | solution.py:113
  664.7 16.4 %copy.64 = f32[2,1,8,4,16,32,32]{5,6,0,4,3,2,1:T(8,128)} copy(f32[2,1,8,4,16,32,32]{6,5,4,2,3,0,1:T(8,128)} %bitcast.217) | data formatting | bytes 8388608 | tf_op jit(solution)/shard_map/all_to_all | solution.py:113
  681.2 57.7 %fusion.6 = bf16[1,32,16,32,256]{4,3,2,1,0:T(8,128)(2,1)} fusion(f32[16,32,256,32]{2,3,1,0:T(8,128)} %fusion.14, f32[2,32,16,32,32]{3,4,0,2,1:T(8,128)} %bitcast.227, f32[32]{0:T(128)S(1)} %copy-done.4, f32[1,32,256]{2,1,0:T(8,128)S(1)} %get-tuple-element.19, f32[1,32,256]{2,1,0:T(8,128)S(1)} %get-tuple-element.20), kind=kOutput, calls=%fused_computation.11 | convolution fusion | flops 3502260224 | bytes 29425792 | tf_op jit(solution)/shard_map/pbcxky,pkz->bcxyz/dot_general | solution.py:14
  (48 shorter events, 57.5 us)
Async XLA Ops:
  6.5 525.3 %copy-start = (bf16[32,32]{1,0:T(8,128)(2,1)S(1)}, bf16[32,32]{1,0:T(8,128)(2,1)}, u32[]{:S(2)}) copy-start(bf16[32,32]{1,0:T(8,128)(2,1)} %param.6) | copy-start | bytes 6148
  6.5 24.2 %copy-start.2 = (bf16[1,32,16,32,256]{4,3,2,1,0:T(8,128)(2,1)S(1)}, bf16[1,32,16,32,256]{4,3,2,1,0:T(8,128)(2,1)}, u32[]{:S(2)}) copy-start(bf16[1,32,16,32,256]{4,3,2,1,0:T(8,128)(2,1)} %param.4) | copy-start | bytes 25165828
  70.8 100.6 %all-to-all-start = ((f32[2,1,32,16,1024]{4,3,1,0,2:T(8,128)}), f32[2,1,32,16,1024]{4,3,1,0,2:T(8,128)}, u32[]{:S(2)}, u32[]{:S(2)}) async-start(f32[2,1,32,16,1024]{4,3,1,0,2:T(8,128)} %pad_maximum_fusion), calls=%async_computation | async-start | bytes 8388608 | tf_op jit(solution)/shard_map/all_to_all | solution.py:61
  78.2 294.0 %all-gather.2.cloned.1.call-start = ((), (), s32[]{:S(2)}) async-start(), calls=%async_computation.4 | async-start | bytes 9437184 | tf_op jit(solution)/shard_map/all_gather | solution.py:74
  383.8 8.4 %copy-start.3 = (f32[64,8,64,32]{2,1,0,3:T(8,128)S(1)}, f32[64,8,64,32]{2,1,0,3:T(8,128)}, u32[]{:S(2)}) copy-start(f32[64,8,64,32]{2,1,0,3:T(8,128)} %get-tuple-element.12) | copy-start | bytes 12582916
  526.9 97.8 %all-to-all-start.3 = ((f32[8,1,131072]{2,1,0:T(1,128)}), f32[8,1,131072]{2,1,0:T(1,128)}, u32[]{:S(2)}, u32[]{:S(2)}) async-start(f32[8,1,131072]{2,1,0:T(1,128)} %reshape.329), calls=%async_computation.3 | async-start | bytes 8388608 | tf_op jit(solution)/shard_map/all_to_all | solution.py:113
  664.7 16.4 %copy-start.4 = (f32[32]{0:T(128)S(1)}, f32[32]{0:T(128)}, u32[]{:S(2)}) copy-start(f32[32]{0:T(128)} %param.7) | copy-start | bytes 388
  681.2 57.7 %copy-start.1 = (bf16[32,32]{1,0:T(8,128)(2,1)S(1)}, bf16[32,32]{1,0:T(8,128)(2,1)}, u32[]{:S(2)}) copy-start(bf16[32,32]{1,0:T(8,128)(2,1)} %param.6) | copy-start | bytes 6148
Sparse Core Ops, SparseCore 0:
  249.5 122.5 all-gather.1
where the time goes:
time: 756 us; the launch traced here: 746 us
  waiting for transfers between devices  295 us (39%)
  matrix products  150 us (20%)
  local copies, waits for them, and re-layouts  139 us (18%)
  other arithmetic  78.1 us (10%)
  blocking collectives  57.8 us (8%)
  between operations  14.2 us (2%)
  starting transfers between devices  12.1 us (2%)
    dot_general x19, matrix products, contract(): jnp.einsum(form, left, right, precision=lax.Precision.HIGHEST, preferred_...  136 us
    all_gather x1, waiting for transfers between devices, body(): gathered = lax.all_gather(spectrum, 'px', axis=2, tiled=True)  123 us
    all_to_all x1, waiting for transfers between devices, body(): lax.all_to_all(along_z, 'px', split_axis=2, concat_axis=3, tiled=True)  93.2 us
    all_to_all x1, waiting for transfers between devices, body(): lax.all_to_all(planes, 'px', split_axis=3, concat_axis=2, tiled=True)  78.7 us
    unnamed x18, local copies, waits for them, and re-layouts  56.6 us
    unnamed x3, other arithmetic  39.1 us
    all_to_all x1, blocking collectives, body(): lax.all_to_all(jnp.stack([back_real, back_imag], axis=0), 'py', split_axi...  28.9 us
    all_to_all x1, blocking collectives, body(): lax.all_to_all(along_x, 'py', split_axis=4, concat_axis=5, tiled=True)  28.9 us
  transfers between devices with their start and end apart: 3, of which 3 were waited for; matrix products, arithmetic and copies ran while one was open for 2% of the time, Pallas kernels for 0%

commit v1 on v0

--- a/solution.py
+++ b/solution.py
@@ -71,7 +71,12 @@
         "bciky,yj->bcikj", moved[0], sin_y
     )
     spectrum = jnp.stack([spec_real, spec_imag], axis=0).astype(jnp.bfloat16)
-    gathered = lax.all_gather(spectrum, "px", axis=2, tiled=True)
+    ring = [spectrum]
+    for hop in range(7):
+        ring.append(lax.ppermute(ring[-1], "px", [(dev, (dev + 1) % 8) for dev in range(8)]))
+    gathered = jnp.roll(
+        jnp.concatenate(ring[::-1], axis=2), (lax.axis_index("px") + 1) * ring[0].shape[2], axis=2
+    )
     in_real = gathered[0].astype(jnp.float32)
     in_imag = gathered[1].astype(jnp.float32)
     weight_real = spectral_weight[0].astype(jnp.float32)

time: 756 us -> 829 us (1.097)
  waiting for transfers between devices: 295 us -> 343 us
  local copies, waits for them, and re-layouts: 139 us -> 168 us
  between operations: 14.2 us -> 0.59 us
    ppermute x0 -> x7, waiting for transfers between devices: none -> 172 us  [body(): lax.ppermute(ring[-1], 'px', [(dev, (dev + 1) % 8) for dev in range(8)])]
    all_gather x1 -> x0, waiting for transfers between devices: 123 us -> none  [body(): gathered = lax.all_gather(spectrum, 'px', axis=2, tiled=True)]
    unnamed x18 -> x50, local copies, waits for them, and re-layouts: 56.6 us -> 86.6 us
    unnamed x3 -> x5, other arithmetic: 39.1 us -> 40.3 us
  transfers between devices with their start and end apart: 3 -> 9, of which waited for: 3 -> 9; matrix products, arithmetic and copies ran while one was open for 2% -> 2% of each run, Pallas kernels for 0% -> 0%
where the time goes in v1:
time: 829 us; the launch traced here: 818 us
  waiting for transfers between devices  343 us (41%)
  local copies, waits for them, and re-layouts  168 us (20%)
  matrix products  154 us (19%)
  other arithmetic  79.5 us (10%)
  blocking collectives  59 us (7%)
  starting transfers between devices  13.6 us (2%)
    ppermute x7, waiting for transfers between devices, body(): lax.ppermute(ring[-1], 'px', [(dev, (dev + 1) % 8) for dev in range(8)])  172 us
    dot_general x19, matrix products, contract(): jnp.einsum(form, left, right, precision=lax.Precision.HIGHEST, preferred_...  140 us
    all_to_all x1, waiting for transfers between devices, body(): lax.all_to_all(along_z, 'px', split_axis=2, concat_axis=3, tiled=True)  93.3 us
    unnamed x50, local copies, waits for them, and re-layouts  86.6 us
    all_to_all x1, waiting for transfers between devices, body(): lax.all_to_all(planes, 'px', split_axis=3, concat_axis=2, tiled=True)  78.5 us
    unnamed x5, other arithmetic  40.3 us
    all_to_all x1, blocking collectives, body(): lax.all_to_all(jnp.stack([back_real, back_imag], axis=0), 'py', split_axi...  30.1 us
    all_to_all x1, blocking collectives, body(): lax.all_to_all(along_x, 'py', split_axis=4, concat_axis=5, tiled=True)  28.9 us
  transfers between devices with their start and end apart: 9, of which 9 were waited for; matrix products, arithmetic and copies ran while one was open for 2% of the time, Pallas kernels for 0%

profile of v1, /device:TPU:0, one launch (start us, length us, event | category | flops | bytes accessed | tf_op | source)
XLA Modules:
  0.0 818.4 jit_solution(16734713008782258587)
XLA Ops:
  0.0 24.2 %convolution_bitcast_fusion.1 = f32[1,32,16,32,32]{4,3,2,1,0:T(8,128)} fusion(bf16[1,32,16,32,256]{4,3,2,1,0:T(8,128)(2,1)} %param.4), kind=kOutput, calls=%fused_computation.41 | convolution fusion | flops 1610727424 | bytes 10485760 | tf_op jit(solution)/shard_map/bcxyz,zk->bcxky/dot_general | solution.py:14
  24.2 21.1 %convolution_bitcast_fusion = f32[1,32,16,32,32]{4,3,2,1,0:T(8,128)} fusion(bf16[1,32,16,32,256]{4,3,2,1,0:T(8,128)(2,1)S(1)} %copy-done.2), kind=kOutput, calls=%fused_computation.40 | convolution fusion | flops 1610735616 | bytes 10485760 | tf_op jit(solution)/shard_map/bcxyz,zk->bcxky/dot_general | solution.py:14
  45.4 6.6 stack.50
  52.0 8.2 stack.51
  64.6 7.3 all-to-all-start
  71.9 93.3 %all-to-all-done = f32[2,1,32,16,1024]{4,3,1,0,2:T(8,128)} async-done(((f32[2,1,32,16,1024]{4,3,1,0,2:T(8,128)}), f32[2,1,32,16,1024]{4,3,1,0,2:T(8,128)}, u32[]{:S(2)}, u32[]{:S(2)}) %all-to-all-start) | async-done | bytes 4194336 | tf_op jit(solution)/shard_map/all_to_all | solution.py:61
  188.2 28.9 %all_to_all.60 = f32[4,1,131072]{2,1,0:T(1,128)} all-to-all(f32[4,1,131072]{2,1,0:T(1,128)S(1)} %reshape.325), channel_id=1, replica_groups=mesh['px'=8,'py'=4] {'py'}, dimensions={0} | all-to-all | bytes 4194304 | tf_op jit(solution)/shard_map/all_to_all | solution.py:64
  217.6 7.6 reduce.8
  246.0 25.8 %collective-permute-done = bf16[2,1,4,64,8,64]{5,4,3,2,1,0:T(8,128)(2,1)S(1)} collective-permute-done((bf16[2,1,4,64,8,64]{5,4,3,2,1,0:T(8,128)(2,1)S(1)}, bf16[2,1,4,64,8,64]{5,4,3,2,1,0:T(8,128)(2,1)S(1)}, u32[]{:S(2)}, u32[]{:S(2)}) %collective-permute-start) | collective-permute-done | bytes 524320 | tf_op jit(solution)/shard_map/ppermute | solution.py:76
  271.8 26.4 %collective-permute-done.1 = bf16[2,1,4,64,8,64]{5,4,3,2,1,0:T(8,128)(2,1)S(1)} collective-permute-done((bf16[2,1,4,64,8,64]{5,4,3,2,1,0:T(8,128)(2,1)S(1)}, bf16[2,1,4,64,8,64]{5,4,3,2,1,0:T(8,128)(2,1)S(1)}, u32[]{:S(2)}, u32[]{:S(2)}) %collective-permute-start.1) | collective-permute-done | bytes 524320 | tf_op jit(solution)/shard_map/ppermute | solution.py:76
  299.1 25.5 %collective-permute-done.2 = bf16[2,1,4,64,8,64]{5,4,3,2,1,0:T(8,128)(2,1)S(1)} collective-permute-done((bf16[2,1,4,64,8,64]{5,4,3,2,1,0:T(8,128)(2,1)S(1)}, bf16[2,1,4,64,8,64]{5,4,3,2,1,0:T(8,128)(2,1)S(1)}, u32[]{:S(2)}, u32[]{:S(2)}) %collective-permute-start.2) | collective-permute-done | bytes 524320 | tf_op jit(solution)/shard_map/ppermute | solution.py:76
  325.7 24.7 %collective-permute-done.3 = bf16[2,1,4,64,8,64]{5,4,3,2,1,0:T(8,128)(2,1)S(1)} collective-permute-done((bf16[2,1,4,64,8,64]{5,4,3,2,1,0:T(8,128)(2,1)S(1)}, bf16[2,1,4,64,8,64]{5,4,3,2,1,0:T(8,128)(2,1)S(1)}, u32[]{:S(2)}, u32[]{:S(2)}) %collective-permute-start.3) | collective-permute-done | bytes 524320 | tf_op jit(solution)/shard_map/ppermute | solution.py:76
  351.3 23.8 %collective-permute-done.4 = bf16[2,1,4,64,8,64]{5,4,3,2,1,0:T(8,128)(2,1)S(1)} collective-permute-done((bf16[2,1,4,64,8,64]{5,4,3,2,1,0:T(8,128)(2,1)S(1)}, bf16[2,1,4,64,8,64]{5,4,3,2,1,0:T(8,128)(2,1)S(1)}, u32[]{:S(2)}, u32[]{:S(2)}) %collective-permute-start.4) | collective-permute-done | bytes 524320 | tf_op jit(solution)/shard_map/ppermute | solution.py:76
  376.1 23.1 %collective-permute-done.5 = bf16[2,1,4,64,8,64]{5,4,3,2,1,0:T(8,128)(2,1)} collective-permute-done((bf16[2,1,4,64,8,64]{5,4,3,2,1,0:T(8,128)(2,1)S(1)}, bf16[2,1,4,64,8,64]{5,4,3,2,1,0:T(8,128)(2,1)}, u32[]{:S(2)}, u32[]{:S(2)}) %collective-permute-start.5) | collective-permute-done | bytes 524320 | tf_op jit(solution)/shard_map/ppermute | solution.py:76
  399.2 22.4 %collective-permute-done.6 = bf16[2,1,4,64,8,64]{5,4,3,2,1,0:T(8,128)(2,1)} collective-permute-done((bf16[2,1,4,64,8,64]{5,4,3,2,1,0:T(8,128)(2,1)}, bf16[2,1,4,64,8,64]{5,4,3,2,1,0:T(8,128)(2,1)}, u32[]{:S(2)}, u32[]{:S(2)}) %collective-permute-start.6) | collective-permute-done | bytes 524320 | tf_op jit(solution)/shard_map/ppermute | solution.py:76
  450.0 11.6 %fusion.16 = (f32[64,8,64,32]{2,1,0,3:T(8,128)}, f32[64,8,64,32]{2,1,0,3:T(8,128)}) fusion(bf16[2,1,64,64,8,64]{5,4,3,2,1,0:T(8,128)(2,1)} %constant_dynamic-update-slice_fusion, s32[]{:T(128)S(6)} %add.156, s32[]{:T(128)S(6)} %select_n.133), kind=kLoop, calls=%fused_computation.32 | loop fusion | flops 2097152 | bytes 12582920
  461.6 8.4 %copy.106 = f32[64,8,64,32]{2,0,1,3:T(8,128)} copy(f32[64,8,64,32]{2,1,0,3:T(8,128)} %get-tuple-element.12) | data formatting | bytes 8388608
  470.0 5.0 copy.107
  475.0 23.1 %fusion.3 = (f32[64,8,64,4]{2,0,1,3:T(8,128)S(1)}, f32[64,8,64,4]{2,0,1,3:T(8,128)S(1)}, f32[64,8,64,4]{2,0,1,3:T(8,128)}, f32[64,8,64,4]{2,0,1,3:T(8,128)S(1)}) fusion(f32[64,8,64,32]{2,0,1,3:T(8,128)} %copy.106, bf16[2,32,4,8,64,64]{5,4,3,2,1,0:T(8,128)(2,1)} %param.5, f32[64,8,64,32]{2,0,1,3:T(8,128)} %copy.107), kind=kLoop, calls=%fused_computation.7 | loop fusion | flops 41418752 | bytes 27262976
  510.7 4.7 copy.58
  519.9 30.1 %all_to_all.61 = f32[4,1,131072]{2,1,0:T(1,128)} all-to-all(f32[4,1,131072]{2,1,0:T(1,128)S(1)} %reshape.327), channel_id=1, replica_groups=mesh['px'=8,'py'=4] {'py'}, dimensions={0} | all-to-all | bytes 4194304 | tf_op jit(solution)/shard_map/all_to_all | solution.py:98
  550.0 7.6 reduce.9
  578.9 14.4 %copy.62 = f32[2,1,4,128,32,32]{5,4,2,1,0,3:T(8,128)} copy(f32[2,1,4,128,32,32]{3,5,4,2,1,0:T(8,128)} %pad_maximum_fusion.2) | data formatting | bytes 8388608 | tf_op jit(solution)/shard_map/stack | solution.py:109
  593.3 12.8 %reshape.329 = f32[8,1,131072]{2,1,0:T(1,128)} reshape(f32[128,2,1,4,32,32]{5,4,3,2,1,0:T(8,128)} %bitcast.215) | data formatting | bytes 8388608
  606.1 4.7 all-to-all-start.3
  611.2 14.2 %fusion.14 = f32[16,32,256,32]{2,3,1,0:T(8,128)} fusion(bf16[32,16,32,256]{3,2,1,0:T(8,128)(2,1)} %bitcast.214, bf16[32,32]{1,0:T(8,128)(2,1)S(1)} %copy-done), kind=kOutput, calls=%fused_computation.29 | convolution fusion | flops 268435456 | bytes 25167872 | tf_op jit(solution)/shard_map/oc,bcxyz->boxyz/dot_general | solution.py:120
  625.4 78.5 %all-to-all-done.3 = f32[8,1,131072]{2,1,0:T(1,128)} async-done(((f32[8,1,131072]{2,1,0:T(1,128)}), f32[8,1,131072]{2,1,0:T(1,128)}, u32[]{:S(2)}, u32[]{:S(2)}) %all-to-all-start.3) | async-done | bytes 4194336 | tf_op jit(solution)/shard_map/all_to_all | solution.py:118
  703.9 14.9 %reduce.10 = f32[8,131072]{1,0:T(8,128)} reduce(f32[8,1,131072]{2,1,0:T(1,128)} %all-to-all-done.3, f32[]{:T(128)} %broadcast.332), dimensions={1}, to_apply=%all_to_all.53.reduce_sub_computation | reduce | bytes 8388612 | tf_op jit(solution)/shard_map/all_to_all | solution.py:118
  718.8 13.3 %reshape.330 = f32[128,2,1,4,32,32]{5,4,3,2,1,0:T(8,128)} reshape(f32[8,131072]{1,0:T(8,128)} %reduce.10) | data formatting | bytes 8388608
  732.1 11.8 %copy.63 = f32[2,1,4,128,32,32]{5,4,3,2,0,1:T(8,128)} copy(f32[2,1,4,128,32,32]{5,4,2,1,0,3:T(8,128)} %bitcast.216) | data formatting | bytes 8388608 | tf_op jit(solution)/shard_map/all_to_all | solution.py:118
  743.9 16.5 %copy.64 = f32[2,1,8,4,16,32,32]{5,6,0,4,3,2,1:T(8,128)} copy(f32[2,1,8,4,16,32,32]{6,5,4,2,3,0,1:T(8,128)} %bitcast.217) | data formatting | bytes 8388608 | tf_op jit(solution)/shard_map/all_to_all | solution.py:118
  760.4 57.7 %fusion.6 = bf16[1,32,16,32,256]{4,3,2,1,0:T(8,128)(2,1)} fusion(f32[16,32,256,32]{2,3,1,0:T(8,128)} %fusion.14, f32[2,32,16,32,32]{3,4,0,2,1:T(8,128)} %bitcast.229, f32[32]{0:T(128)S(1)} %copy-done.11, f32[1,32,256]{2,1,0:T(8,128)S(1)} %sine_multiply_fusion, f32[1,32,256]{2,1,0:T(8,128)S(1)} %cosine_multiply_fusion), kind=kOutput, calls=%fused_computation.11 | convolution fusion | flops 3502260224 | bytes 29425792 | tf_op jit(solution)/shard_map/pbcxky,pkz->bcxyz/dot_general | solution.py:14
  (94 shorter events, 119.4 us)
Async XLA Ops:
  0.0 611.1 %copy-start = (bf16[32,32]{1,0:T(8,128)(2,1)S(1)}, bf16[32,32]{1,0:T(8,128)(2,1)}, u32[]{:S(2)}) copy-start(bf16[32,32]{1,0:T(8,128)(2,1)} %param.6) | copy-start | bytes 6148
  0.0 24.2 %copy-start.2 = (bf16[1,32,16,32,256]{4,3,2,1,0:T(8,128)(2,1)S(1)}, bf16[1,32,16,32,256]{4,3,2,1,0:T(8,128)(2,1)}, u32[]{:S(2)}) copy-start(bf16[1,32,16,32,256]{4,3,2,1,0:T(8,128)(2,1)} %param.4) | copy-start | bytes 25165828
  64.6 100.6 %all-to-all-start = ((f32[2,1,32,16,1024]{4,3,1,0,2:T(8,128)}), f32[2,1,32,16,1024]{4,3,1,0,2:T(8,128)}, u32[]{:S(2)}, u32[]{:S(2)}) async-start(f32[2,1,32,16,1024]{4,3,1,0,2:T(8,128)} %pad_maximum_fusion), calls=%async_computation | async-start | bytes 8388608 | tf_op jit(solution)/shard_map/all_to_all | solution.py:61
  244.5 27.3 %collective-permute-start = (bf16[2,1,4,64,8,64]{5,4,3,2,1,0:T(8,128)(2,1)S(1)}, bf16[2,1,4,64,8,64]{5,4,3,2,1,0:T(8,128)(2,1)S(1)}, u32[]{:S(2)}, u32[]{:S(2)}) collective-permute-start(bf16[2,1,4,64,8,64]{5,4,3,2,1,0:T(8,128)(2,1)S(1)} %pad_maximum_fusion.4), channel_id=1, source_target_pairs={{0,4},{4,8},{8,12},{12,16},{16,20},{20,24},{24,28},{28,0},{1,5},{5... | collective-permute-start | bytes 1572872 | tf_op jit(solution)/shard_map/ppermute | solution.py:76
  271.8 26.4 %collective-permute-start.1 = (bf16[2,1,4,64,8,64]{5,4,3,2,1,0:T(8,128)(2,1)S(1)}, bf16[2,1,4,64,8,64]{5,4,3,2,1,0:T(8,128)(2,1)S(1)}, u32[]{:S(2)}, u32[]{:S(2)}) collective-permute-start(bf16[2,1,4,64,8,64]{5,4,3,2,1,0:T(8,128)(2,1)S(1)} %collective-permute-done), channel_id=1, source_target_pairs={{0,4},{4,8},{8,12},{12,16},{16,20},{20,24},{24,28},{28,0},{1,5},{5... | collective-permute-start | bytes 1572872 | tf_op jit(solution)/shard_map/ppermute | solution.py:76
  298.1 1.0 copy-start.3
  299.1 25.5 %collective-permute-start.2 = (bf16[2,1,4,64,8,64]{5,4,3,2,1,0:T(8,128)(2,1)S(1)}, bf16[2,1,4,64,8,64]{5,4,3,2,1,0:T(8,128)(2,1)S(1)}, u32[]{:S(2)}, u32[]{:S(2)}) collective-permute-start(bf16[2,1,4,64,8,64]{5,4,3,2,1,0:T(8,128)(2,1)S(1)} %collective-permute-done.1), channel_id=1, source_target_pairs={{0,4},{4,8},{8,12},{12,16},{16,20},{20,24},{24,28},{28,0},{1,5},{5... | collective-permute-start | bytes 1572872 | tf_op jit(solution)/shard_map/ppermute | solution.py:76
  324.7 1.0 copy-start.5
  325.7 24.7 %collective-permute-start.3 = (bf16[2,1,4,64,8,64]{5,4,3,2,1,0:T(8,128)(2,1)S(1)}, bf16[2,1,4,64,8,64]{5,4,3,2,1,0:T(8,128)(2,1)S(1)}, u32[]{:S(2)}, u32[]{:S(2)}) collective-permute-start(bf16[2,1,4,64,8,64]{5,4,3,2,1,0:T(8,128)(2,1)S(1)} %collective-permute-done.2), channel_id=1, source_target_pairs={{0,4},{4,8},{8,12},{12,16},{16,20},{20,24},{24,28},{28,0},{1,5},{5... | collective-permute-start | bytes 1572872 | tf_op jit(solution)/shard_map/ppermute | solution.py:76
  350.3 1.0 copy-start.7
  351.3 23.8 %collective-permute-start.4 = (bf16[2,1,4,64,8,64]{5,4,3,2,1,0:T(8,128)(2,1)S(1)}, bf16[2,1,4,64,8,64]{5,4,3,2,1,0:T(8,128)(2,1)S(1)}, u32[]{:S(2)}, u32[]{:S(2)}) collective-permute-start(bf16[2,1,4,64,8,64]{5,4,3,2,1,0:T(8,128)(2,1)S(1)} %collective-permute-done.3), channel_id=1, source_target_pairs={{0,4},{4,8},{8,12},{12,16},{16,20},{20,24},{24,28},{28,0},{1,5},{5... | collective-permute-start | bytes 1572872 | tf_op jit(solution)/shard_map/ppermute | solution.py:76
  375.1 1.0 copy-start.9
  376.1 23.1 %collective-permute-start.5 = (bf16[2,1,4,64,8,64]{5,4,3,2,1,0:T(8,128)(2,1)S(1)}, bf16[2,1,4,64,8,64]{5,4,3,2,1,0:T(8,128)(2,1)}, u32[]{:S(2)}, u32[]{:S(2)}) collective-permute-start(bf16[2,1,4,64,8,64]{5,4,3,2,1,0:T(8,128)(2,1)S(1)} %collective-permute-done.4), channel_id=1, source_target_pairs={{0,4},{4,8},{8,12},{12,16},{16,20},{20,24},{24,28},{28,0},{1,5},{5... | collective-permute-start | bytes 1572872 | tf_op jit(solution)/shard_map/ppermute | solution.py:76
  399.2 22.4 %collective-permute-start.6 = (bf16[2,1,4,64,8,64]{5,4,3,2,1,0:T(8,128)(2,1)}, bf16[2,1,4,64,8,64]{5,4,3,2,1,0:T(8,128)(2,1)}, u32[]{:S(2)}, u32[]{:S(2)}) collective-permute-start(bf16[2,1,4,64,8,64]{5,4,3,2,1,0:T(8,128)(2,1)} %collective-permute-done.5), channel_id=1, source_target_pairs={{0,4},{4,8},{8,12},{12,16},{16,20},{20,24},{24,28},{28,0},{1,5},{5... | collective-permute-start | bytes 1572872 | tf_op jit(solution)/shard_map/ppermute | solution.py:76
  399.2 43.8 %copy-start.10 = (bf16[2,1,4,64,8,64]{5,4,3,2,1,0:T(8,128)(2,1)S(1)}, bf16[2,1,4,64,8,64]{5,4,3,2,1,0:T(8,128)(2,1)}, u32[]{:S(2)}) copy-start(bf16[2,1,4,64,8,64]{5,4,3,2,1,0:T(8,128)(2,1)} %copy-done.9) | copy-start | bytes 1572868
  399.2 45.0 %copy-start.8 = (bf16[2,1,4,64,8,64]{5,4,3,2,1,0:T(8,128)(2,1)S(1)}, bf16[2,1,4,64,8,64]{5,4,3,2,1,0:T(8,128)(2,1)}, u32[]{:S(2)}) copy-start(bf16[2,1,4,64,8,64]{5,4,3,2,1,0:T(8,128)(2,1)} %copy-done.7) | copy-start | bytes 1572868
  399.2 46.1 %copy-start.6 = (bf16[2,1,4,64,8,64]{5,4,3,2,1,0:T(8,128)(2,1)S(1)}, bf16[2,1,4,64,8,64]{5,4,3,2,1,0:T(8,128)(2,1)}, u32[]{:S(2)}) copy-start(bf16[2,1,4,64,8,64]{5,4,3,2,1,0:T(8,128)(2,1)} %copy-done.5) | copy-start | bytes 1572868
  399.2 47.3 %copy-start.4 = (bf16[2,1,4,64,8,64]{5,4,3,2,1,0:T(8,128)(2,1)S(1)}, bf16[2,1,4,64,8,64]{5,4,3,2,1,0:T(8,128)(2,1)}, u32[]{:S(2)}) copy-start(bf16[2,1,4,64,8,64]{5,4,3,2,1,0:T(8,128)(2,1)} %copy-done.3) | copy-start | bytes 1572868
  461.6 8.4 %slice-start = ((s8[8388608]{0:T(1024)(128)(4,1)}), s8[4194304]{0:T(1024)(128)(4,1)S(1)}, s32[]{:S(2)}) async-start(s8[8388608]{0:T(1024)(128)(4,1)} %bitcast.218), calls=%async_computation.4 | async-start | bytes 8388608
  461.6 8.4 %slice-start.1 = ((s8[8388608]{0:T(1024)(128)(4,1)}), s8[4194304]{0:T(1024)(128)(4,1)S(1)}, s32[]{:S(2)}) async-start(s8[8388608]{0:T(1024)(128)(4,1)} %bitcast.218), calls=%async_computation.5 | async-start | bytes 8388608
  606.1 97.8 %all-to-all-start.3 = ((f32[8,1,131072]{2,1,0:T(1,128)}), f32[8,1,131072]{2,1,0:T(1,128)}, u32[]{:S(2)}, u32[]{:S(2)}) async-start(f32[8,1,131072]{2,1,0:T(1,128)} %reshape.329), calls=%async_computation.3 | async-start | bytes 8388608 | tf_op jit(solution)/shard_map/all_to_all | solution.py:118
  743.9 16.5 %copy-start.11 = (f32[32]{0:T(128)S(1)}, f32[32]{0:T(128)}, u32[]{:S(2)}) copy-start(f32[32]{0:T(128)} %param.7) | copy-start | bytes 388
  760.4 57.7 %copy-start.1 = (bf16[32,32]{1,0:T(8,128)(2,1)S(1)}, bf16[32,32]{1,0:T(8,128)(2,1)}, u32[]{:S(2)}) copy-start(bf16[32,32]{1,0:T(8,128)(2,1)} %param.6) | copy-start | bytes 6148
